TPU v7x, 512 devices: a whole 4x4x16 slice. The times are simulated.
512 devices in a mesh: tm: 16 (over z_lo, x), chan: 32 (over z_hi, y, core).
Axes of the slice: x: 4, y: 4, z: 16 (z_hi: 4, z_lo: 4; z = z_hi * 4 + z_lo), core: 2. Of those that a mesh axis runs over, the one named last changes fastest.
Arguments:
- voltages: bfloat16 [2, 128, 2048, 1024], P(None, 'tm', 'chan'), may hold values from -6 to 6
- subspace: float32 [32, 64, 32, 1024], P('chan', 'tm'), may hold values from -0.1875 to 0.1875
- order: int32 [64], replicated, may hold values from 0 to 63, each once
- beam_seeds: int32 [256], replicated, may hold values from 1 to 65520
- flagged: int32 [16], replicated, may hold values from 0 to 511
Outputs:
- beams: bfloat16 [2, 32, 64, 512, 128], P(None, None, 'tm', 'chan')
- tracked: float32 [32, 64, 32, 1024], P('chan', 'tm')
Inputs may be any that keep to these rules, and one draw needn't show every extreme that they name: `order`: each of 0 to 63 once. `flagged`: station numbers; a station may occur more than once.
All inputs are finite; a program needn't handle non-finite values.
Results may differ from a plain program's by a relative error of at most 0.0084.
Values may be sent and summed in bfloat16 or wider, within the bound.
No kernel may reach another device: no remote copies, remote signals or barrier semaphores. Data moves between devices by JAX's collectives and lax.ppermute only.
A program may use at most 64 MiB of HBM per device.

v0:
```python
import math
import jax
import jax.numpy as jnp
from jax import lax
from jax.sharding import PartitionSpec as P

CH = 2048
SUB = 2
TWO_PI = 2.0 * math.pi


def beam_weights(beam_seeds, channels, stations, total_channels):
    station_no = jnp.arange(stations, dtype=jnp.int32) + 1
    delays = (station_no[:, None] * beam_seeds[None, :] % 65521).astype(jnp.float32) / 65521.0
    frequency = 1.0 + channels.astype(jnp.float32) / total_channels
    angles = delays[None, :, :] * (TWO_PI * frequency)[:, None, None]
    factor = 1.0 / math.sqrt(stations)
    cosine = jnp.cos(angles) * factor
    sine_part = jnp.sin(angles) * factor
    upper = jnp.concatenate([cosine, sine_part], axis=2)
    under = jnp.concatenate([-sine_part, cosine], axis=2)
    return jnp.concatenate([upper, under], axis=1).astype(jnp.bfloat16)


def power_step(voltage_input, tracked, steering_weight):
    sample_count = voltage_input.shape[0]
    coarse_channel = tracked.astype(jnp.bfloat16)
    projected_input = jnp.einsum(
        "xbj,bqj->bxq", voltage_input, coarse_channel, preferred_element_type=jnp.float32
    ).astype(jnp.bfloat16)
    beam_image = (
        jnp.einsum(
            "nwg,wny->ngy", projected_input, voltage_input, preferred_element_type=jnp.float32
        )
        + sample_count * tracked
    )
    gram = jnp.einsum("crs,cks->crk", beam_image, beam_image, precision=lax.Precision.HIGHEST)
    lower = jnp.linalg.cholesky(gram)
    tracked = jax.scipy.linalg.solve_triangular(lower, beam_image, lower=True)
    subspace_vectors = tracked.astype(jnp.bfloat16)
    lengthwise_axis = jnp.einsum(
        "xbj,bqj->bxq", voltage_input, subspace_vectors, preferred_element_type=jnp.float32
    ).astype(jnp.bfloat16)
    mixing = jnp.einsum(
        "crs,csb->crb", subspace_vectors, steering_weight, preferred_element_type=jnp.float32
    ).astype(jnp.bfloat16)
    direct_output = jnp.einsum(
        "edi,diy->dye", voltage_input, steering_weight, preferred_element_type=jnp.float32
    )
    beams = direct_output - jnp.einsum(
        "ctr,crb->cbt", lengthwise_axis, mixing, preferred_element_type=jnp.float32
    )
    return (tracked, beams.astype(jnp.bfloat16))


def per_device(voltages, subspace, order, beam_seeds, flagged):
    signals = voltages.shape[-1]
    stations = signals // 2
    slots = subspace.shape[1]
    per_group = order.shape[0]
    marks = jnp.any(flagged[:, None] == jnp.arange(stations, dtype=jnp.int32)[None, :], axis=0)
    keep = jnp.where(marks, 0.0, 1.0).astype(jnp.bfloat16)
    keep = jnp.concatenate([keep, keep])
    ordered = jnp.take(voltages, order, axis=2) * keep
    group = lax.axis_index("chan")
    first_slot = lax.axis_index("tm") * slots
    chosen = lax.dynamic_slice_in_dim(order, first_slot, slots)
    channels = group * per_group + chosen
    steering_weight = beam_weights(beam_seeds, channels, stations, CH)
    state = subspace[0]
    results = []
    for part in range(SUB):
        turned = lax.all_to_all(ordered[part], "tm", split_axis=1, concat_axis=0, tiled=True)
        state, formed = power_step(turned, state, steering_weight)
        results.append(
            lax.all_to_all(formed[None], "chan", split_axis=2, concat_axis=0, tiled=True)
        )
    output = jnp.stack(results)
    return (output, state[None])


def solution(mesh):
    return jax.shard_map(
        per_device,
        mesh=mesh,
        in_specs=(P(None, "tm", "chan", None), P("chan", "tm", None, None), P(), P(), P()),
        out_specs=(P(None, None, "tm", "chan", None), P("chan", "tm", None, None)),
        check_vma=False,
    )
```

profile of v0, /device:TPU:12, one launch (start us, length us, event | category | flops | bytes accessed | tf_op | source)
XLA Modules:
  0.0 212.0 jit_solution(4434291030982119377)
XLA Ops:
  0.6 0.0 copy-start
  0.6 0.8 compare_select_fusion
  1.5 0.7 compare_and_fusion
  2.1 0.7 fusion.50
  2.9 7.9 %gather_fusion = bf16[64,2,8,1024]{3,0,2,1:T(8,128)(2,1)} fusion(bf16[2,8,64,1024]{3,2,1,0:T(8,128)(2,1)S(1)} %copy-done, s32[1024]{0:T(1024)S(1)} %pad_clamp_fusion), kind=kCustom, calls=%fused_computation | custom fusion | bytes 4194560 | tf_op jit(solution)/shard_map/jit(_take)/gather | solution.py:64
  10.8 1.8 multiply_bitcast_fusion
  12.7 1.1 slice_bitcast_fusion.1
  13.8 1.5 copy.37
  15.4 8.9 %all-to-all-start = ((bf16[8,64,1024]{2,0,1:T(8,128)(2,1)}), bf16[8,64,1024]{2,0,1:T(8,128)(2,1)S(1)}, u32[]{:S(2)}, u32[]{:S(2)}) async-start(bf16[8,64,1024]{2,0,1:T(8,128)(2,1)} %copy.37), calls=%async_computation | async-start | bytes 2097152 | tf_op jit(solution)/shard_map/all_to_all | solution.py:73
  24.3 2.8 %copy.44 = bf16[8,64,1024]{2,0,1:T(8,128)(2,1)} copy(bf16[8,64,1024]{2,1,0:T(8,128)(2,1)} %get-tuple-element.5) | data formatting | bytes 2097152 | tf_op jit(solution)/shard_map/squeeze | solution.py:73
  27.1 21.2 %all-to-all-done = bf16[8,64,1024]{2,0,1:T(8,128)(2,1)S(1)} async-done(((bf16[8,64,1024]{2,0,1:T(8,128)(2,1)}), bf16[8,64,1024]{2,0,1:T(8,128)(2,1)S(1)}, u32[]{:S(2)}, u32[]{:S(2)}) %all-to-all-start) | async-done | bytes 1048608 | tf_op jit(solution)/shard_map/all_to_all | solution.py:73
  48.3 1.0 copy-done.1
  49.2 6.9 %all-to-all-start.2 = ((bf16[8,64,1024]{2,0,1:T(8,128)(2,1)}), bf16[8,64,1024]{2,0,1:T(8,128)(2,1)S(1)}, u32[]{:S(2)}, u32[]{:S(2)}) async-start(bf16[8,64,1024]{2,0,1:T(8,128)(2,1)} %copy.44), calls=%async_computation.2 | async-start | bytes 2097152 | tf_op jit(solution)/shard_map/all_to_all | solution.py:73
  56.1 0.1 add_multiply_fusion
  56.2 0.4 fusion.33
  56.6 9.1 %fusion.4 = (bf16[4,512,256]{1,2,0:T(8,128)(2,1)}, bf16[4,512,256]{1,2,0:T(8,128)(2,1)}, bf16[4,512,256]{1,2,0:T(8,128)(2,1)}) fusion(f32[4]{0:T(128)S(1)} %add_multiply_fusion, f32[512,256]{0,1:T(8,128)S(1)} %fusion.33), kind=kLoop, calls=%fused_computation.8 | loop fusion | flops 3670016 | bytes 3670032 | tf_op jit(solution)/shard_map/convert.5
  65.7 3.3 %convolution_add_fusion.1 = f32[4,32,1024]{2,1,0:T(8,128)} fusion(bf16[8,16,4,1024]{3,0,2,1:T(8,128)(2,1)} %bitcast.82, f32[1,4,32,1024]{3,2,1,0:T(8,128)} %param.9), kind=kOutput, calls=%fused_computation.18 | convolution fusion | flops 67518464 | bytes 2097152 | tf_op jit(solution)/shard_map/nwg,wny->ngy/dot_general | solution.py:32
  69.0 1.8 fusion.56
  70.9 0.1 copy.39
  71.0 11.7 %custom-call.8 = f32[4,32,32]{2,1,0:T(8,128)S(1)} custom-call(f32[4,32,32]{2,1,0:T(8,128)S(1)} %fusion.49), custom_call_target="Cholesky" | custom-call | tf_op jit(solution)/shard_map/jit(cholesky)/cholesky | solution.py:38
  82.7 0.1 compare_reduce_fusion.1
  82.8 0.1 select_bitcast_fusion.1
  82.9 9.8 %custom-call.9 = f32[4,1,32,32]{2,3,1,0:T(8,128)S(1)} custom-call(f32[4,1,32,32]{3,2,1,0:T(8,128)S(1)} %select_bitcast_fusion.1), custom_call_target="InvertDiagBlocksLowerTriangular" | custom-call | tf_op jit(solution)/shard_map/jit(_solve_triangular)/vmap()/triangular_solve | solution.py:39
  92.8 1.7 fusion.47
  94.5 0.8 copy-done.3
  95.3 3.7 %convolution_convert_fusion.1 = bf16[4,32,512]{2,1,0:T(8,128)(2,1)S(1)} fusion(f32[4,32,1024]{2,1,0:T(8,128)S(1)} %fusion.47, bf16[4,512,256]{1,2,0:T(8,128)(2,1)} %get-tuple-element.8, bf16[4,512,256]{1,2,0:T(8,128)(2,1)} %get-tuple-element.7, bf16[4,512,256]{1,2,0:T(8,128)(2,1)} %get-tuple-element.6), kind=kOutput, calls=%fused_computation.20 | convolution fusion | flops 151191552 | bytes 3801088 | tf_op jit(solution)/shard_map/crs,csb->crb/dot_general | solution.py:44
  99.0 2.2 %fusion.20 = f32[4,512,128]{2,1,0:T(8,128)} fusion(bf16[8,16,4,1024]{3,0,2,1:T(8,128)(2,1)S(1)} %bitcast.84, bf16[4,512,256]{1,2,0:T(8,128)(2,1)S(1)} %copy-done.9, bf16[4,512,256]{1,2,0:T(8,128)(2,1)S(1)} %copy-done.7, bf16[4,512,256]{1,2,0:T(8,128)(2,1)S(1)} %copy-done.5), kind=kOutput, calls=%fused_computation.34 | convolution fusion | flops 553648128 | bytes 5242880 | tf_op jit(solution)/shard_map/edi,diy->dye/dot_general | solution.py:47
  101.2 3.2 %fusion.9 = bf16[1,4,512,128]{3,2,1,0:T(8,128)(2,1)} fusion(f32[4,512,128]{2,1,0:T(8,128)} %fusion.20, bf16[4,32,512]{2,1,0:T(8,128)(2,1)S(1)} %convolution_convert_fusion.1, bf16[8,16,4,1024]{3,0,2,1:T(8,128)(2,1)} %bitcast.83, f32[4,32,1024]{2,1,0:T(8,128)} %copy-done.3), kind=kOutput, calls=%fused_computation.16 | convolution fusion | flops 51003392 | bytes 3276800 | tf_op jit(solution)/shard_map/ctr,crb->cbt/dot_general | solution.py:50
  104.5 2.2 %copy.42 = bf16[1,4,512,128]{3,1,0,2:T(4,128)(2,1)} copy(bf16[1,4,512,128]{3,2,1,0:T(8,128)(2,1)} %fusion.9) | data formatting | bytes 1048576 | tf_op jit(solution)/shard_map/broadcast_in_dim | solution.py:76
  106.7 15.7 %all-to-all-start.1 = ((bf16[1,4,512,128]{3,1,0,2:T(4,128)(2,1)}), bf16[1,4,512,128]{3,1,0,2:T(4,128)(2,1)}, u32[]{:S(2)}, u32[]{:S(2)}) async-start(bf16[1,4,512,128]{3,1,0,2:T(4,128)(2,1)} %copy.42), calls=%async_computation.1 | async-start | bytes 1048576 | tf_op jit(solution)/shard_map/all_to_all | solution.py:76
  122.4 2.7 %convolution_add_fusion = f32[4,32,1024]{2,1,0:T(8,128)} fusion(bf16[8,16,4,1024]{3,0,2,1:T(8,128)(2,1)S(1)} %bitcast.79, f32[4,32,1024]{2,1,0:T(8,128)} %copy-done.3), kind=kOutput, calls=%fused_computation.17 | convolution fusion | flops 67518464 | bytes 2097152 | tf_op jit(solution)/shard_map/nwg,wny->ngy/dot_general | solution.py:32
  125.1 1.8 fusion.57
  127.0 0.1 copy.46
  127.1 11.7 %custom-call.10 = f32[4,32,32]{2,1,0:T(8,128)S(1)} custom-call(f32[4,32,32]{2,1,0:T(8,128)S(1)} %fusion.46), custom_call_target="Cholesky" | custom-call | tf_op jit(solution)/shard_map/jit(cholesky)/cholesky | solution.py:38
  138.8 0.1 compare_reduce_fusion
  139.0 0.1 select_bitcast_fusion
  139.0 9.8 %custom-call.11 = f32[4,1,32,32]{2,3,1,0:T(8,128)S(1)} custom-call(f32[4,1,32,32]{3,2,1,0:T(8,128)S(1)} %select_bitcast_fusion), custom_call_target="InvertDiagBlocksLowerTriangular" | custom-call | tf_op jit(solution)/shard_map/jit(_solve_triangular)/vmap()/triangular_solve | solution.py:39
  148.9 1.7 fusion.44
  150.6 0.8 copy-done.4
  151.4 3.7 %convolution_convert_fusion = bf16[4,32,512]{2,1,0:T(8,128)(2,1)S(1)} fusion(f32[4,32,1024]{2,1,0:T(8,128)S(1)} %fusion.44, bf16[4,512,256]{1,2,0:T(8,128)(2,1)} %get-tuple-element.8, bf16[4,512,256]{1,2,0:T(8,128)(2,1)} %get-tuple-element.7, bf16[4,512,256]{1,2,0:T(8,128)(2,1)} %get-tuple-element.6), kind=kOutput, calls=%fused_computation.19 | convolution fusion | flops 151191552 | bytes 3801088 | tf_op jit(solution)/shard_map/crs,csb->crb/dot_general | solution.py:44
  155.1 2.3 %fusion.14 = f32[4,512,128]{2,1,0:T(8,128)} fusion(bf16[8,16,4,1024]{3,0,2,1:T(8,128)(2,1)S(1)} %bitcast.80, bf16[4,512,256]{1,2,0:T(8,128)(2,1)S(1)} %copy-done.10, bf16[4,512,256]{1,2,0:T(8,128)(2,1)S(1)} %copy-done.8, bf16[4,512,256]{1,2,0:T(8,128)(2,1)S(1)} %copy-done.6), kind=kOutput, calls=%fused_computation.30 | convolution fusion | flops 553648128 | bytes 5242880 | tf_op jit(solution)/shard_map/edi,diy->dye/dot_general | solution.py:47
  157.4 2.9 %fusion.8 = bf16[1,4,512,128]{3,2,1,0:T(8,128)(2,1)} fusion(f32[4,512,128]{2,1,0:T(8,128)} %fusion.14, bf16[4,32,512]{2,1,0:T(8,128)(2,1)S(1)} %convolution_convert_fusion, bf16[8,16,4,1024]{3,0,2,1:T(8,128)(2,1)S(1)} %bitcast.81, f32[4,32,1024]{2,1,0:T(8,128)} %copy-done.4), kind=kOutput, calls=%fused_computation.15 | convolution fusion | flops 51003392 | bytes 3276800 | tf_op jit(solution)/shard_map/ctr,crb->cbt/dot_general | solution.py:50
  160.3 2.2 %copy.49 = bf16[1,4,512,128]{3,1,0,2:T(4,128)(2,1)} copy(bf16[1,4,512,128]{3,2,1,0:T(8,128)(2,1)} %fusion.8) | data formatting | bytes 1048576 | tf_op jit(solution)/shard_map/broadcast_in_dim | solution.py:76
  162.5 14.6 %all-to-all-start.3 = ((bf16[1,4,512,128]{3,1,0,2:T(4,128)(2,1)}), bf16[1,4,512,128]{3,1,0,2:T(4,128)(2,1)S(1)}, u32[]{:S(2)}, u32[]{:S(2)}) async-start(bf16[1,4,512,128]{3,1,0,2:T(4,128)(2,1)} %copy.49), calls=%async_computation.3 | async-start | bytes 1048576 | tf_op jit(solution)/shard_map/all_to_all | solution.py:76
  177.1 1.1 copy.90
  178.2 32.6 %all-to-all-done.3 = bf16[1,4,512,128]{3,1,0,2:T(4,128)(2,1)S(1)} async-done(((bf16[1,4,512,128]{3,1,0,2:T(4,128)(2,1)}), bf16[1,4,512,128]{3,1,0,2:T(4,128)(2,1)S(1)}, u32[]{:S(2)}, u32[]{:S(2)}) %all-to-all-start.3) | async-done | bytes 524320 | tf_op jit(solution)/shard_map/all_to_all | solution.py:76
  210.8 0.1 copy.89
  210.9 1.1 pad_maximum_fusion
  (34 shorter events, 0.2 us)
Async XLA Ops:
  0.6 2.3 %copy-start = (bf16[2,8,64,1024]{3,2,1,0:T(8,128)(2,1)S(1)}, bf16[2,8,64,1024]{3,2,1,0:T(8,128)(2,1)}, u32[]{:S(2)}) copy-start(bf16[2,8,64,1024]{3,2,1,0:T(8,128)(2,1)} %param.8) | copy-start | bytes 6291460
  15.4 32.9 %all-to-all-start = ((bf16[8,64,1024]{2,0,1:T(8,128)(2,1)}), bf16[8,64,1024]{2,0,1:T(8,128)(2,1)S(1)}, u32[]{:S(2)}, u32[]{:S(2)}) async-start(bf16[8,64,1024]{2,0,1:T(8,128)(2,1)} %copy.37), calls=%async_computation | async-start | bytes 2097152 | tf_op jit(solution)/shard_map/all_to_all | solution.py:73
  24.2 31.9 %copy-start.12 = (s32[64]{0:T(128)S(1)}, s32[64]{0:T(128)}, u32[]{:S(2)}) copy-start(s32[64]{0:T(128)} %param.10) | copy-start | bytes 772
  24.3 32.0 %copy-start.11 = (s32[256]{0:T(256)S(1)}, s32[256]{0:T(256)}, u32[]{:S(2)}) copy-start(s32[256]{0:T(256)} %param.11) | copy-start | bytes 3076
  48.3 1.0 copy-start.1
  49.2 57.5 %all-to-all-start.2 = ((bf16[8,64,1024]{2,0,1:T(8,128)(2,1)}), bf16[8,64,1024]{2,0,1:T(8,128)(2,1)S(1)}, u32[]{:S(2)}, u32[]{:S(2)}) async-start(bf16[8,64,1024]{2,0,1:T(8,128)(2,1)} %copy.44), calls=%async_computation.2 | async-start | bytes 2097152 | tf_op jit(solution)/shard_map/all_to_all | solution.py:73
  94.5 0.8 copy-start.3
  95.3 3.7 %copy-start.2 = (bf16[8,64,1024]{2,0,1:T(8,128)(2,1)S(1)}, bf16[8,64,1024]{2,0,1:T(8,128)(2,1)}, u32[]{:S(2)}) copy-start(bf16[8,64,1024]{2,0,1:T(8,128)(2,1)} %copy-done.1) | copy-start | bytes 3145732
  95.3 3.7 %copy-start.5 = (bf16[4,512,256]{1,2,0:T(8,128)(2,1)S(1)}, bf16[4,512,256]{1,2,0:T(8,128)(2,1)}, u32[]{:S(2)}) copy-start(bf16[4,512,256]{1,2,0:T(8,128)(2,1)} %get-tuple-element.6) | copy-start | bytes 3145732
  95.3 3.7 %copy-start.7 = (bf16[4,512,256]{1,2,0:T(8,128)(2,1)S(1)}, bf16[4,512,256]{1,2,0:T(8,128)(2,1)}, u32[]{:S(2)}) copy-start(bf16[4,512,256]{1,2,0:T(8,128)(2,1)} %get-tuple-element.7) | copy-start | bytes 3145732
  95.3 3.7 %copy-start.9 = (bf16[4,512,256]{1,2,0:T(8,128)(2,1)S(1)}, bf16[4,512,256]{1,2,0:T(8,128)(2,1)}, u32[]{:S(2)}) copy-start(bf16[4,512,256]{1,2,0:T(8,128)(2,1)} %get-tuple-element.8) | copy-start | bytes 3145732
  106.7 55.8 %all-to-all-start.1 = ((bf16[1,4,512,128]{3,1,0,2:T(4,128)(2,1)}), bf16[1,4,512,128]{3,1,0,2:T(4,128)(2,1)}, u32[]{:S(2)}, u32[]{:S(2)}) async-start(bf16[1,4,512,128]{3,1,0,2:T(4,128)(2,1)} %copy.42), calls=%async_computation.1 | async-start | bytes 1048576 | tf_op jit(solution)/shard_map/all_to_all | solution.py:76
  150.6 0.8 copy-start.4
  151.4 3.7 %copy-start.6 = (bf16[4,512,256]{1,2,0:T(8,128)(2,1)S(1)}, bf16[4,512,256]{1,2,0:T(8,128)(2,1)}, u32[]{:S(2)}) copy-start(bf16[4,512,256]{1,2,0:T(8,128)(2,1)} %get-tuple-element.6) | copy-start | bytes 3145732
  151.4 3.7 %copy-start.8 = (bf16[4,512,256]{1,2,0:T(8,128)(2,1)S(1)}, bf16[4,512,256]{1,2,0:T(8,128)(2,1)}, u32[]{:S(2)}) copy-start(bf16[4,512,256]{1,2,0:T(8,128)(2,1)} %get-tuple-element.7) | copy-start | bytes 3145732
  151.4 3.7 %copy-start.10 = (bf16[4,512,256]{1,2,0:T(8,128)(2,1)S(1)}, bf16[4,512,256]{1,2,0:T(8,128)(2,1)}, u32[]{:S(2)}) copy-start(bf16[4,512,256]{1,2,0:T(8,128)(2,1)} %get-tuple-element.8) | copy-start | bytes 3145732
  162.5 48.3 %all-to-all-start.3 = ((bf16[1,4,512,128]{3,1,0,2:T(4,128)(2,1)}), bf16[1,4,512,128]{3,1,0,2:T(4,128)(2,1)S(1)}, u32[]{:S(2)}, u32[]{:S(2)}) async-start(bf16[1,4,512,128]{3,1,0,2:T(4,128)(2,1)} %copy.49), calls=%async_computation.3 | async-start | bytes 1048576 | tf_op jit(solution)/shard_map/all_to_all | solution.py:76
where the time goes:
time: 213 us; the launch traced here: 212 us
  other arithmetic  58.4 us (27%)
  waiting for transfers between devices  53.8 us (25%)
  starting transfers between devices  46 us (22%)
  matrix products  31 us (15%)
  local copies, waits for them, and re-layouts  21.9 us (10%)
    all_to_all x2, waiting for transfers between devices, per_device(): lax.all_to_all(formed[None], 'chan', split_axis=2, concat_axis=0, tiled=T...  32.6 us
    all_to_all x2, starting transfers between devices, per_device(): lax.all_to_all(formed[None], 'chan', split_axis=2, concat_axis=0, tiled=T...  30.3 us
    another operation x7, other arithmetic, power_step(): lower = jnp.linalg.cholesky(gram)  23.8 us
    all_to_all x2, waiting for transfers between devices, per_device(): lax.all_to_all(ordered[part], 'tm', split_axis=1, concat_axis=0, tiled=True)  21.2 us
    another operation x5, other arithmetic, power_step(): tracked = jax.scipy.linalg.solve_triangular(lower, beam_image, lower=True)  19.9 us
    all_to_all x2, starting transfers between devices, per_device(): lax.all_to_all(ordered[part], 'tm', split_axis=1, concat_axis=0, tiled=True)  15.8 us
    another operation x1, other arithmetic  9.12 us
    gather x1, local copies, waits for them, and re-layouts, per_device(): ordered = jnp.take(voltages, order, axis=2) * keep  7.92 us
  transfers between devices with their start and end apart: 4, of which 2 were waited for; matrix products, arithmetic and copies ran while one was open for 44% of the time, Pallas kernels for 0%

commit v1 on v0

--- a/solution.py
+++ b/solution.py
@@ -70,7 +70,12 @@
     state = subspace[0]
     results = []
     for part in range(SUB):
-        turned = lax.all_to_all(ordered[part], "tm", split_axis=1, concat_axis=0, tiled=True)
+        turned = jnp.concatenate(
+            lax.all_to_all(
+                jnp.stack(jnp.split(ordered[part], lax.axis_size("tm"), axis=1)), "tm", 0, 0
+            ),
+            axis=0,
+        )
         state, formed = power_step(turned, state, steering_weight)
         results.append(
             lax.all_to_all(formed[None], "chan", split_axis=2, concat_axis=0, tiled=True)

time: 213 us -> 219 us (1.028)
  the two profiles are of different devices: /device:TPU:12 before, /device:TPU:18 now
where the time goes in v1:
time: 219 us; the launch traced here: 217 us
  other arithmetic  58.4 us (27%)
  local copies, waits for them, and re-layouts  50 us (23%)
  starting transfers between devices  46.6 us (21%)
  waiting for transfers between devices  32.6 us (15%)
  matrix products  29 us (13%)
    unnamed x54, local copies, waits for them, and re-layouts  33.8 us
    all_to_all x2, waiting for transfers between devices, per_device(): lax.all_to_all(formed[None], 'chan', split_axis=2, concat_axis=0, tiled=T...  32.6 us
    all_to_all x2, starting transfers between devices, per_device(): lax.all_to_all(formed[None], 'chan', split_axis=2, concat_axis=0, tiled=T...  30.2 us
    another operation x7, other arithmetic, power_step(): lower = jnp.linalg.cholesky(gram)  23.8 us
    another operation x5, other arithmetic, power_step(): tracked = jax.scipy.linalg.solve_triangular(lower, beam_image, lower=True)  19.9 us
    all_to_all x2, starting transfers between devices, per_device(): lax.all_to_all(jnp.stack(jnp.split(ordered[part], lax.axis_size('tm'), ax...  16.4 us
    another operation x1, other arithmetic  9.1 us
    gather x1, local copies, waits for them, and re-layouts, per_device(): ordered = jnp.take(voltages, order, axis=2) * keep  7.93 us
  transfers between devices with their start and end apart: 4, of which 1 were waited for; matrix products, arithmetic and copies ran while one was open for 51% of the time, Pallas kernels for 0%

profile of v1, /device:TPU:18, one launch (start us, length us, event | category | flops | bytes accessed | tf_op | source)
XLA Modules:
  0.0 217.5 jit_solution(1377130113008513899)
XLA Ops:
  0.6 0.8 compare_select_fusion
  2.1 0.7 fusion.82
  2.9 7.9 %gather_fusion = bf16[64,2,8,1024]{3,0,2,1:T(8,128)(2,1)} fusion(bf16[2,8,64,1024]{3,2,1,0:T(8,128)(2,1)S(1)} %copy-done, s32[1024]{0:T(1024)S(1)} %pad_clamp_fusion), kind=kCustom, calls=%fused_computation | custom fusion | bytes 4194560 | tf_op jit(solution)/shard_map/jit(_take)/gather | solution.py:64
  10.8 1.8 multiply_bitcast_fusion
  12.7 1.2 slice_bitcast_fusion.1
  15.8 0.7 fusion.72
  22.3 0.7 fusion.62
  24.3 8.9 %all-to-all-start = ((bf16[16,8,4,1024]{3,2,1,0:T(4,128)(2,1)}), bf16[16,8,4,1024]{3,2,1,0:T(4,128)(2,1)S(1)}, u32[]{:S(2)}, u32[]{:S(2)}) async-start(bf16[16,8,4,1024]{3,2,1,0:T(4,128)(2,1)} %fusion.60), calls=%async_computation | async-start | bytes 2097152 | tf_op jit(solution)/shard_map/all_to_all | solution.py:74
  33.2 1.6 fusion.59
  34.7 1.6 fusion.58
  36.3 1.5 fusion.57
  37.8 1.6 fusion.56
  39.4 1.5 fusion.55
  40.9 1.6 fusion.54
  42.5 1.5 fusion.53
  44.0 1.5 fusion.52
  45.6 1.6 fusion.51
  47.1 1.6 fusion.50
  48.7 1.5 fusion.49
  50.2 1.6 fusion.48
  51.8 1.5 fusion.47
  53.3 1.6 fusion.46
  54.9 1.6 fusion.45
  56.4 1.6 fusion.44
  58.0 7.5 %all-to-all-start.2 = ((bf16[16,8,4,1024]{3,2,1,0:T(4,128)(2,1)}), bf16[16,8,4,1024]{3,2,1,0:T(4,128)(2,1)}, u32[]{:S(2)}, u32[]{:S(2)}) async-start(bf16[16,8,4,1024]{3,2,1,0:T(4,128)(2,1)} %fusion.44), calls=%async_computation.2 | async-start | bytes 2097152 | tf_op jit(solution)/shard_map/all_to_all | solution.py:74
  66.0 9.1 %fusion.4 = (bf16[4,512,256]{1,2,0:T(8,128)(2,1)}, bf16[4,512,256]{1,2,0:T(8,128)(2,1)}, bf16[4,512,256]{1,2,0:T(8,128)(2,1)}) fusion(f32[4]{0:T(128)S(1)} %add_multiply_fusion, f32[512,256]{0,1:T(8,128)S(1)} %fusion.33), kind=kLoop, calls=%fused_computation.8 | loop fusion | flops 3670016 | bytes 3670032 | tf_op jit(solution)/shard_map/convert.5
  75.1 3.1 %convolution_add_fusion.1 = f32[4,32,1024]{2,1,0:T(8,128)} fusion(bf16[16,8,4,1024]{3,2,1,0:T(4,128)(2,1)S(1)} %all-to-all-done, f32[1,4,32,1024]{3,2,1,0:T(8,128)} %param.9), kind=kOutput, calls=%fused_computation.18 | convolution fusion | flops 67518464 | bytes 2097152 | tf_op jit(solution)/shard_map/nwg,wny->ngy/dot_general | solution.py:32
  78.2 1.8 fusion.88
  80.2 11.7 %custom-call.8 = f32[4,32,32]{2,1,0:T(8,128)S(1)} custom-call(f32[4,32,32]{2,1,0:T(8,128)S(1)} %fusion.81), custom_call_target="Cholesky" | custom-call | tf_op jit(solution)/shard_map/jit(cholesky)/cholesky | solution.py:38
  92.1 9.8 %custom-call.9 = f32[4,1,32,32]{2,3,1,0:T(8,128)S(1)} custom-call(f32[4,1,32,32]{3,2,1,0:T(8,128)S(1)} %select_bitcast_fusion.1), custom_call_target="InvertDiagBlocksLowerTriangular" | custom-call | tf_op jit(solution)/shard_map/jit(_solve_triangular)/vmap()/triangular_solve | solution.py:39
  102.0 1.7 fusion.79
  103.7 0.8 copy-done.1
  104.5 3.7 %convolution_convert_fusion.1 = bf16[4,32,512]{2,1,0:T(8,128)(2,1)S(1)} fusion(f32[4,32,1024]{2,1,0:T(8,128)S(1)} %fusion.79, bf16[4,512,256]{1,2,0:T(8,128)(2,1)} %get-tuple-element.8, bf16[4,512,256]{1,2,0:T(8,128)(2,1)} %get-tuple-element.7, bf16[4,512,256]{1,2,0:T(8,128)(2,1)} %get-tuple-element.6), kind=kOutput, calls=%fused_computation.20 | convolution fusion | flops 151191552 | bytes 3801088 | tf_op jit(solution)/shard_map/crs,csb->crb/dot_general | solution.py:44
  108.2 2.4 %fusion.20 = f32[4,512,128]{2,1,0:T(8,128)} fusion(bf16[16,8,4,1024]{3,2,1,0:T(4,128)(2,1)S(1)} %all-to-all-done, bf16[4,512,256]{1,2,0:T(8,128)(2,1)S(1)} %copy-done.8, bf16[4,512,256]{1,2,0:T(8,128)(2,1)S(1)} %copy-done.6, bf16[4,512,256]{1,2,0:T(8,128)(2,1)S(1)} %copy-done.4), kind=kOutput, calls=%fused_computation.34 | convolution fusion | flops 553648128 | bytes 5242880 | tf_op jit(solution)/shard_map/edi,diy->dye/dot_general | solution.py:47
  110.6 2.9 %fusion.9 = bf16[1,4,512,128]{3,2,1,0:T(8,128)(2,1)} fusion(f32[4,512,128]{2,1,0:T(8,128)} %fusion.20, bf16[4,32,512]{2,1,0:T(8,128)(2,1)S(1)} %convolution_convert_fusion.1, bf16[16,8,4,1024]{3,2,1,0:T(4,128)(2,1)S(1)} %all-to-all-done, f32[4,32,1024]{2,1,0:T(8,128)} %copy-done.1), kind=kOutput, calls=%fused_computation.16 | convolution fusion | flops 51003392 | bytes 3276800 | tf_op jit(solution)/shard_map/ctr,crb->cbt/dot_general | solution.py:50
  113.5 2.3 %copy.39 = bf16[1,4,512,128]{3,1,0,2:T(4,128)(2,1)} copy(bf16[1,4,512,128]{3,2,1,0:T(8,128)(2,1)} %fusion.9) | data formatting | bytes 1048576 | tf_op jit(solution)/shard_map/broadcast_in_dim | solution.py:81
  115.8 15.6 %all-to-all-start.1 = ((bf16[1,4,512,128]{3,1,0,2:T(4,128)(2,1)}), bf16[1,4,512,128]{3,1,0,2:T(4,128)(2,1)}, u32[]{:S(2)}, u32[]{:S(2)}) async-start(bf16[1,4,512,128]{3,1,0,2:T(4,128)(2,1)} %copy.39), calls=%async_computation.1 | async-start | bytes 1048576 | tf_op jit(solution)/shard_map/all_to_all | solution.py:81
  131.4 2.6 %convolution_add_fusion = f32[4,32,1024]{2,1,0:T(8,128)S(1)} fusion(bf16[16,8,4,1024]{3,2,1,0:T(4,128)(2,1)} %all-to-all-done.2, f32[4,32,1024]{2,1,0:T(8,128)S(1)} %copy-done.2), kind=kOutput, calls=%fused_computation.17 | convolution fusion | flops 67518464 | bytes 2097152 | tf_op jit(solution)/shard_map/nwg,wny->ngy/dot_general | solution.py:32
  134.8 11.7 %custom-call.10 = f32[4,32,32]{2,1,0:T(8,128)S(1)} custom-call(f32[4,32,32]{2,1,0:T(8,128)S(1)} %fusion.78), custom_call_target="Cholesky" | custom-call | tf_op jit(solution)/shard_map/jit(cholesky)/cholesky | solution.py:38
  146.7 9.8 %custom-call.11 = f32[4,1,32,32]{2,3,1,0:T(8,128)S(1)} custom-call(f32[4,1,32,32]{3,2,1,0:T(8,128)S(1)} %select_bitcast_fusion), custom_call_target="InvertDiagBlocksLowerTriangular" | custom-call | tf_op jit(solution)/shard_map/jit(_solve_triangular)/vmap()/triangular_solve | solution.py:39
  157.3 3.7 %convolution_convert_fusion = bf16[4,32,512]{2,1,0:T(8,128)(2,1)S(1)} fusion(f32[4,32,1024]{2,1,0:T(8,128)S(1)} %fusion.76, bf16[4,512,256]{1,2,0:T(8,128)(2,1)} %get-tuple-element.8, bf16[4,512,256]{1,2,0:T(8,128)(2,1)} %get-tuple-element.7, bf16[4,512,256]{1,2,0:T(8,128)(2,1)} %get-tuple-element.6), kind=kOutput, calls=%fused_computation.19 | convolution fusion | flops 151191552 | bytes 3801088 | tf_op jit(solution)/shard_map/crs,csb->crb/dot_general | solution.py:44
  161.1 3.5 %fusion.14 = f32[4,512,128]{2,1,0:T(8,128)} fusion(bf16[16,8,4,1024]{3,2,1,0:T(4,128)(2,1)} %all-to-all-done.2, bf16[4,512,256]{1,2,0:T(8,128)(2,1)S(1)} %copy-done.9, bf16[4,512,256]{1,2,0:T(8,128)(2,1)S(1)} %copy-done.7, bf16[4,512,256]{1,2,0:T(8,128)(2,1)S(1)} %copy-done.5), kind=kOutput, calls=%fused_computation.30 | convolution fusion | flops 553648128 | bytes 5242880 | tf_op jit(solution)/shard_map/edi,diy->dye/dot_general | solution.py:47
  164.6 2.2 %fusion.8 = bf16[1,4,512,128]{3,2,1,0:T(8,128)(2,1)S(1)} fusion(f32[4,512,128]{2,1,0:T(8,128)} %fusion.14, bf16[4,32,512]{2,1,0:T(8,128)(2,1)S(1)} %convolution_convert_fusion, bf16[16,8,4,1024]{3,2,1,0:T(4,128)(2,1)} %all-to-all-done.2, f32[4,32,1024]{2,1,0:T(8,128)S(1)} %fusion.76), kind=kOutput, calls=%fused_computation.15 | convolution fusion | flops 51003392 | bytes 3276800 | tf_op jit(solution)/shard_map/ctr,crb->cbt/dot_general | solution.py:50
  166.8 1.2 copy.45
  168.0 14.6 %all-to-all-start.3 = ((bf16[1,4,512,128]{3,1,0,2:T(4,128)(2,1)}), bf16[1,4,512,128]{3,1,0,2:T(4,128)(2,1)S(1)}, u32[]{:S(2)}, u32[]{:S(2)}) async-start(bf16[1,4,512,128]{3,1,0,2:T(4,128)(2,1)} %copy.45), calls=%async_computation.3 | async-start | bytes 1048576 | tf_op jit(solution)/shard_map/all_to_all | solution.py:81
  182.6 1.1 copy.86
  183.7 32.6 %all-to-all-done.3 = bf16[1,4,512,128]{3,1,0,2:T(4,128)(2,1)S(1)} async-done(((bf16[1,4,512,128]{3,1,0,2:T(4,128)(2,1)}), bf16[1,4,512,128]{3,1,0,2:T(4,128)(2,1)S(1)}, u32[]{:S(2)}, u32[]{:S(2)}) %all-to-all-start.3) | async-done | bytes 524320 | tf_op jit(solution)/shard_map/all_to_all | solution.py:81
  216.4 1.1 pad_maximum_fusion
  (62 shorter events, 12.2 us)
Async XLA Ops:
  0.6 2.3 %copy-start = (bf16[2,8,64,1024]{3,2,1,0:T(8,128)(2,1)S(1)}, bf16[2,8,64,1024]{3,2,1,0:T(8,128)(2,1)}, u32[]{:S(2)}) copy-start(bf16[2,8,64,1024]{3,2,1,0:T(8,128)(2,1)} %param.8) | copy-start | bytes 6291460
  24.3 33.7 %all-to-all-start = ((bf16[16,8,4,1024]{3,2,1,0:T(4,128)(2,1)}), bf16[16,8,4,1024]{3,2,1,0:T(4,128)(2,1)S(1)}, u32[]{:S(2)}, u32[]{:S(2)}) async-start(bf16[16,8,4,1024]{3,2,1,0:T(4,128)(2,1)} %fusion.60), calls=%async_computation | async-start | bytes 2097152 | tf_op jit(solution)/shard_map/all_to_all | solution.py:74
  33.2 32.4 %copy-start.11 = (s32[64]{0:T(128)S(1)}, s32[64]{0:T(128)}, u32[]{:S(2)}) copy-start(s32[64]{0:T(128)} %param.10) | copy-start | bytes 772
  33.2 32.5 %copy-start.10 = (s32[256]{0:T(256)S(1)}, s32[256]{0:T(256)}, u32[]{:S(2)}) copy-start(s32[256]{0:T(256)} %param.11) | copy-start | bytes 3076
  58.0 57.8 %all-to-all-start.2 = ((bf16[16,8,4,1024]{3,2,1,0:T(4,128)(2,1)}), bf16[16,8,4,1024]{3,2,1,0:T(4,128)(2,1)}, u32[]{:S(2)}, u32[]{:S(2)}) async-start(bf16[16,8,4,1024]{3,2,1,0:T(4,128)(2,1)} %fusion.44), calls=%async_computation.2 | async-start | bytes 2097152 | tf_op jit(solution)/shard_map/all_to_all | solution.py:74
  103.7 0.8 copy-start.1
  104.5 3.7 %copy-start.4 = (bf16[4,512,256]{1,2,0:T(8,128)(2,1)S(1)}, bf16[4,512,256]{1,2,0:T(8,128)(2,1)}, u32[]{:S(2)}) copy-start(bf16[4,512,256]{1,2,0:T(8,128)(2,1)} %get-tuple-element.6) | copy-start | bytes 3145732
  104.5 3.7 %copy-start.6 = (bf16[4,512,256]{1,2,0:T(8,128)(2,1)S(1)}, bf16[4,512,256]{1,2,0:T(8,128)(2,1)}, u32[]{:S(2)}) copy-start(bf16[4,512,256]{1,2,0:T(8,128)(2,1)} %get-tuple-element.7) | copy-start | bytes 3145732
  104.5 3.7 %copy-start.8 = (bf16[4,512,256]{1,2,0:T(8,128)(2,1)S(1)}, bf16[4,512,256]{1,2,0:T(8,128)(2,1)}, u32[]{:S(2)}) copy-start(bf16[4,512,256]{1,2,0:T(8,128)(2,1)} %get-tuple-element.8) | copy-start | bytes 3145732
  113.5 17.9 %copy-start.2 = (f32[4,32,1024]{2,1,0:T(8,128)S(1)}, f32[4,32,1024]{2,1,0:T(8,128)}, u32[]{:S(2)}) copy-start(f32[4,32,1024]{2,1,0:T(8,128)} %copy-done.1) | copy-start | bytes 1572868
  115.8 52.2 %all-to-all-start.1 = ((bf16[1,4,512,128]{3,1,0,2:T(4,128)(2,1)}), bf16[1,4,512,128]{3,1,0,2:T(4,128)(2,1)}, u32[]{:S(2)}, u32[]{:S(2)}) async-start(bf16[1,4,512,128]{3,1,0,2:T(4,128)(2,1)} %copy.39), calls=%async_computation.1 | async-start | bytes 1048576 | tf_op jit(solution)/shard_map/all_to_all | solution.py:81
  157.3 7.3 %copy-start.3 = (f32[4,32,1024]{2,1,0:T(8,128)}, f32[4,32,1024]{2,1,0:T(8,128)S(1)}, u32[]{:S(2)}) copy-start(f32[4,32,1024]{2,1,0:T(8,128)S(1)} %fusion.76) | copy-start | bytes 1572868
  157.3 3.8 %copy-start.5 = (bf16[4,512,256]{1,2,0:T(8,128)(2,1)S(1)}, bf16[4,512,256]{1,2,0:T(8,128)(2,1)}, u32[]{:S(2)}) copy-start(bf16[4,512,256]{1,2,0:T(8,128)(2,1)} %get-tuple-element.6) | copy-start | bytes 3145732
  157.3 3.8 %copy-start.7 = (bf16[4,512,256]{1,2,0:T(8,128)(2,1)S(1)}, bf16[4,512,256]{1,2,0:T(8,128)(2,1)}, u32[]{:S(2)}) copy-start(bf16[4,512,256]{1,2,0:T(8,128)(2,1)} %get-tuple-element.7) | copy-start | bytes 3145732
  157.3 3.8 %copy-start.9 = (bf16[4,512,256]{1,2,0:T(8,128)(2,1)S(1)}, bf16[4,512,256]{1,2,0:T(8,128)(2,1)}, u32[]{:S(2)}) copy-start(bf16[4,512,256]{1,2,0:T(8,128)(2,1)} %get-tuple-element.8) | copy-start | bytes 3145732
  168.0 48.3 %all-to-all-start.3 = ((bf16[1,4,512,128]{3,1,0,2:T(4,128)(2,1)}), bf16[1,4,512,128]{3,1,0,2:T(4,128)(2,1)S(1)}, u32[]{:S(2)}, u32[]{:S(2)}) async-start(bf16[1,4,512,128]{3,1,0,2:T(4,128)(2,1)} %copy.45), calls=%async_computation.3 | async-start | bytes 1048576 | tf_op jit(solution)/shard_map/all_to_all | solution.py:81
